TPU v7x, 32 devices: a whole 2x2x4 slice. The times are simulated.
32 devices in a mesh: lat: 8 (over y, x, core), chan: 4 (over z).
Axes of the slice: x: 2, y: 2, z: 4, core: 2. Of those that a mesh axis runs over, the one named last changes fastest.
Arguments:
- field: bfloat16 [40, 642, 544], P('lat', None, 'chan'), may hold values from -6 to 6
- cotangent: bfloat16 [40, 642, 1024], P('lat'), may hold values from -6 to 6
- weight: bfloat16 [544, 1024], P('chan'), may hold values from -0.25 to 0.25
- lon_counts: int32 [40], P('lat'), may hold values from 20 to 5136, as said below
- point_mask: int32 [40, 5136], P('lat', 'chan'), may hold values 0 or 1
Outputs:
- field_grad: bfloat16 [40, 642, 544], P('lat', None, 'chan')
- weight_grad: float32 [1024, 544], P('lat', 'chan')
Inputs may be any that keep to these rules, and one draw needn't show every extreme that they name: `lon_counts`: number of longitudes in use in a row; points from there to the end of the row are padding.
All inputs are finite; a program needn't handle non-finite values. No bound on the sum of `point_mask` on one device may be relied on, other than what follows from the above.
Results may differ from a plain program's by a relative error of at most 0.001.
Values sent between devices are 32-bit elements; how exact they have to be, the bound alone decides.
A program may use at most 64 MiB of HBM per device.

v0:
```python
import jax
import jax.numpy as jnp
from jax import lax
from jax.sharding import PartitionSpec as P

P_SIZE = 8


def local(field, cotangent, weight, lon_counts, point_mask):
    row_count, patch_count, features = field.shape
    channels = features // P_SIZE
    full_mask = lax.all_gather(point_mask, "chan", axis=1, tiled=True)
    positions = lax.broadcasted_iota(jnp.int32, full_mask.shape, 1)
    valid = jnp.where(positions < lon_counts[:, None], full_mask, 0)
    total = lax.psum(jnp.sum(valid), "lat")
    scale = lax.rsqrt(jnp.maximum(total.astype(jnp.float32), 1.0))
    point_valid = valid.reshape(row_count, patch_count, 1, P_SIZE)
    masked = (
        field.reshape(row_count, patch_count, channels, P_SIZE) * point_valid.astype(jnp.bfloat16)
    ).reshape(row_count, patch_count, features)
    outcome = lax.dot_general(
        cotangent, weight, (((2,), (1,)), ((), ())), preferred_element_type=jnp.float32
    )
    field_grad = (
        (
            outcome.reshape(row_count, patch_count, channels, P_SIZE)
            * point_valid.astype(jnp.float32)
        )
        .reshape(row_count, patch_count, features)
        .astype(jnp.bfloat16)
    )
    summed = lax.dot_general(
        cotangent, masked, (((0, 1), (0, 1)), ((), ())), preferred_element_type=jnp.float32
    )
    weight_grad = lax.psum_scatter(summed * scale, "lat", scatter_dimension=0, tiled=True)
    return (field_grad, weight_grad)


def solution(mesh):
    in_specs = (
        P("lat", None, "chan"),
        P("lat", None, None),
        P("chan", None),
        P("lat"),
        P("lat", "chan"),
    )
    out_specs = (P("lat", None, "chan"), P("lat", "chan"))
    return jax.shard_map(local, mesh=mesh, in_specs=in_specs, out_specs=out_specs, check_vma=False)
```

profile of v0, /device:TPU:0, one launch (start us, length us, event | category | flops | bytes accessed | tf_op | source)
XLA Modules:
  0.0 79.9 jit_solution(1350397564111324862)
XLA Ops:
  7.2 0.0 copy-start
  7.2 0.0 reduce-scatter.2.cloned.1.call-start
  7.2 15.7 %all-gather = s32[4,1284,5]{1,2,0:T(8,128)S(1)} all-gather(s32[1,1284,5]{1,2,0:T(8,128)} %bitcast.33), channel_id=1, replica_groups=mesh['lat'=8,'chan'=4] {'chan'}, dimensions={0}, use_global_device_ids=true | all-gather | bytes 128400 | tf_op jit(solution)/shard_map/all_gather | solution.py:12
  22.9 0.1 reshape.29
  23.1 1.4 %fusion.5 = (s32[]{:T(128)}, bf16[5,5136]{1,0:T(8,128)(2,1)S(1)}, f32[5,5136]{1,0:T(8,128)S(1)}) fusion(s32[5136,5]{0,1:T(8,128)S(1)} %reshape.29, s32[5]{0:T(128)} %param.8), kind=kLoop, calls=%fused_computation.10 | loop fusion | flops 128399 | bytes 256824 | tf_op jit(solution)/shard_map/reduce_sum | solution.py:15
  24.5 8.6 %psum.7 = s32[]{:T(128)} all-reduce(s32[]{:T(128)} %get-tuple-element.2), channel_id=1, replica_groups=mesh['lat'=8,'chan'=4] {'lat'}, use_global_device_ids=true, to_apply=%region_1.2 | all-reduce | flops 1 | bytes 8 | tf_op jit(solution)/shard_map/psum | solution.py:15
  33.8 0.8 %convert_element_type.32 = bf16[5,642,8]{2,1,0:T(8,128)(2,1)S(1)} reshape(bf16[5,5136]{1,0:T(8,128)(2,1)S(1)} %get-tuple-element.3) | data formatting | bytes 102720 | tf_op jit(solution)/shard_map/convert_element_type | solution.py:19
  34.6 0.3 copy.12
  35.0 5.3 %fusion.2 = f32[1024,136]{0,1:T(8,128)} fusion(bf16[5,642,1024]{2,1,0:T(8,128)(2,1)} %param.6, bf16[5,642,136]{1,2,0:T(8,128)(2,1)} %param.5, bf16[5,642,8]{1,2,0:T(8,128)(2,1)S(1)} %copy.12, f32[]{:T(128)S(6)} %rsqrt.3), kind=kOutput, calls=%fused_computation.4 | convolution fusion | flops 894650688 | bytes 8055620 | tf_op jit(solution)/shard_map/dot_general | solution.py:32
  40.2 0.0 reduce-scatter.2.cloned.1.call-update
  40.2 0.7 convert_element_type.29
  41.0 0.5 copy.11
  41.5 0.0 copy-done
  41.5 6.0 %fusion = bf16[5,642,136]{1,2,0:T(8,128)(2,1)} fusion(bf16[5,642,1024]{2,1,0:T(8,128)(2,1)} %param.6, f32[5,642,8]{1,2,0:T(8,128)S(1)} %copy.11, bf16[136,1024]{1,0:T(8,128)(2,1)S(1)} %copy-done), kind=kOutput, calls=%fused_computation.1 | convolution fusion | flops 894947968 | bytes 7828448 | tf_op jit(solution)/shard_map/dot_general | solution.py:21
  47.5 25.5 %reduce-scatter.2.cloned.1.call-done = f32[128,136]{0,1:T(8,128)} async-done(((f32[1024,136]{0,1:T(8,128)}), f32[128,136]{0,1:T(8,128)}) %reduce-scatter.2.cloned.1.call-update) | async-done | bytes 69648 | tf_op jit(solution)/shard_map/reduce_scatter | solution.py:35
  (1 shorter events, 0.0 us)
Async XLA Ops:
  7.2 34.3 %copy-start = (bf16[136,1024]{1,0:T(8,128)(2,1)S(1)}, bf16[136,1024]{1,0:T(8,128)(2,1)}, u32[]{:S(2)}) copy-start(bf16[136,1024]{1,0:T(8,128)(2,1)} %param.7) | copy-start | bytes 835588
  7.2 65.9 %reduce-scatter.2.cloned.1.call-start = ((), (), s32[]{:S(2)}) async-start(), calls=%async_computation.1 | async-start | bytes 626688 | tf_op jit(solution)/shard_map/reduce_scatter | solution.py:35
Sparse Core Ops, SparseCore 0:
  40.4 32.6 reduce-scatter.1
where the time goes:
time: 80.1 us; the launch traced here: 79.9 us
  waiting for transfers between devices  25.5 us (32%)
  blocking collectives  24.3 us (30%)
  between operations  14.8 us (18%)
  matrix products  11.3 us (14%)
  local copies, waits for them, and re-layouts  2.58 us (3%)
  other arithmetic  1.4 us (2%)
    reduce_scatter x1, waiting for transfers between devices, local(): lax.psum_scatter(summed * scale, 'lat', scatter_dimension=0, tiled=True)  25.5 us
    all_gather x1, blocking collectives, local(): full_mask = lax.all_gather(point_mask, 'chan', axis=1, tiled=True)  15.7 us
    psum x1, blocking collectives, local(): total = lax.psum(jnp.sum(valid), 'lat')  8.65 us
    dot_general x1, matrix products, local(): lax.dot_general(cotangent, weight, (((2,), (1,)), ((), ())), preferred_el...  6.02 us
    dot_general x1, matrix products, local(): lax.dot_general(cotangent, masked, (((0, 1), (0, 1)), ((), ())), preferre...  5.26 us
  transfers between devices with their start and end apart: 1, of which 1 were waited for; matrix products, arithmetic and copies ran while one was open for 9% of the time, Pallas kernels for 0%

commit v1 on v0

--- a/solution.py
+++ b/solution.py
@@ -1,12 +1,224 @@
+import functools
+
 import jax
 import jax.numpy as jnp
 from jax import lax
+from jax.experimental import pallas as pl
+from jax.experimental.pallas import tpu as pltpu
 from jax.sharding import PartitionSpec as P
 
 P_SIZE = 8
-
-
-def local(field, cotangent, weight, lon_counts, point_mask):
+LANES = 128
+MESH = pl.DeviceIdType.MESH
+
+
+def round_up(value, multiple):
+    return (value + multiple - 1) // multiple * multiple
+
+
+def kernel(
+    n_lat, n_chan,
+    field_hbm, cot_hbm, weight_hbm, lon_ref, mask_hbm,
+    grad_ref, wgrad_ref,
+    cot, field, weight, masks, expand, spread, masked,
+    part, pair_recv, chip_sum, chip_recv, count_send, count_recv,
+    cot_sem, load_sem, mask_send, mask_recv, count_ssem, count_rsem,
+    pair_ssem, pair_rsem, chip_ssem, chip_rsem,
+):
+    rows, features, patches = field.shape
+    width = masks.shape[2]
+    n_chips = n_lat // 2
+    owned = wgrad_ref.shape[1]
+    lat, chan = lax.axis_index("lat"), lax.axis_index("chan")
+    chip, core = lat // 2, lax.rem(lat, 2)
+    partner = chip * 2 + 1 - core
+
+    load_mask = pltpu.make_async_copy(mask_hbm, masks.at[chan], load_sem.at[0])
+    load_mask.start()
+    load_weight = pltpu.make_async_copy(weight_hbm, weight, load_sem.at[1])
+    load_weight.start()
+    for r in range(rows):
+        pltpu.make_async_copy(cot_hbm.at[r], cot.at[r], cot_sem.at[r]).start()
+    load_field = pltpu.make_async_copy(field_hbm, field, load_sem.at[2])
+    load_field.start()
+
+    barrier = pltpu.get_barrier_semaphore()
+    for o in range(1, n_chan):
+        pl.semaphore_signal(barrier, inc=1, device_id=(lat, lax.rem(chan + o, n_chan)), device_id_type=MESH)
+    for o in range(1, n_lat):
+        pl.semaphore_signal(barrier, inc=1, device_id=(lax.rem(lat + o, n_lat), chan), device_id_type=MESH)
+
+    lane_of = lax.broadcasted_iota(jnp.int32, spread.shape[1:], 0)
+    patch_of = lax.broadcasted_iota(jnp.int32, spread.shape[1:], 1)
+    shifts = sorted({z * width % P_SIZE for z in range(n_chan)})
+    for index, shift in enumerate(shifts):
+        spread[index] = jnp.where((lane_of + shift) // P_SIZE == patch_of, 1.0, 0.0).astype(jnp.bfloat16)
+
+    load_mask.wait()
+    pl.semaphore_wait(barrier, n_chan + n_lat - 2)
+    mask_copies = []
+    for o in range(1, n_chan):
+        copy = pltpu.make_async_remote_copy(
+            src_ref=masks.at[chan], dst_ref=masks.at[chan],
+            send_sem=mask_send.at[o - 1], recv_sem=mask_recv.at[o - 1],
+            device_id=(lat, lax.rem(chan + o, n_chan)), device_id_type=MESH,
+        )
+        copy.start()
+        mask_copies.append(copy)
+
+    load_weight.wait()
+
+    @pl.loop(0, rows)
+    def _(r):
+        pltpu.make_async_copy(cot_hbm.at[r], cot.at[r], cot_sem.at[r]).wait()
+        grad_ref[r] = lax.dot_general(
+            weight[...], cot[r], (((1,), (1,)), ((), ())), preferred_element_type=jnp.float32
+        ).astype(jnp.bfloat16)
+
+    for copy in mask_copies:
+        copy.wait()
+
+    padded = expand.shape[1]
+    lane = lax.broadcasted_iota(jnp.int32, (P_SIZE, width), 1)
+    sub = lax.broadcasted_iota(jnp.int32, (P_SIZE, width), 0)
+    counts = jnp.zeros((1, width), jnp.int32)
+    valid_all = jnp.zeros((rows * P_SIZE, padded), jnp.float32)
+    for z in range(n_chan):
+        first, shift = z * width // P_SIZE, z * width % P_SIZE
+        pick = lax.rem(lane + shift, P_SIZE) == sub
+        position = lane[:1] + z * width
+        block = masks[z]
+        placed = []
+        for r in range(rows):
+            valid = jnp.where(position < lon_ref[r], block[r:r + 1], 0)
+            counts = counts + valid
+            placed.append(jnp.where(pick, jnp.broadcast_to(valid, (P_SIZE, width)), 0))
+        left = jnp.concatenate(placed, axis=0).astype(jnp.float32).astype(jnp.bfloat16)
+        local = jnp.dot(left, spread[shifts.index(shift)], preferred_element_type=jnp.float32)
+        if padded > local.shape[1]:
+            local = jnp.concatenate(
+                [local, jnp.zeros((rows * P_SIZE, padded - local.shape[1]), jnp.float32)], axis=1
+            )
+        valid_all = valid_all + (pltpu.roll(local, first, axis=1) if first else local)
+    expand[...] = valid_all
+    total_here = jnp.sum(counts)
+    count_send[...] = jnp.full(count_send.shape, total_here, jnp.int32)
+
+    load_field.wait()
+    for r in range(rows):
+        valid8 = expand[r * P_SIZE:(r + 1) * P_SIZE, :patches]
+        tiled = jnp.concatenate([valid8] * (features // P_SIZE), axis=0).astype(jnp.bfloat16)
+        masked[r] = field[r] * tiled
+        grad_ref[r] = grad_ref[r] * tiled
+
+    count_copies = []
+    for o in range(1, n_lat):
+        copy = pltpu.make_async_remote_copy(
+            src_ref=count_send, dst_ref=count_recv.at[o - 1],
+            send_sem=count_ssem.at[o - 1], recv_sem=count_rsem.at[o - 1],
+            device_id=(lax.rem(lat + o, n_lat), chan), device_id_type=MESH,
+        )
+        copy.start()
+        count_copies.append(copy)
+
+    def pair_copy(s):
+        return pltpu.make_async_remote_copy(
+            src_ref=part.at[1 - core, s], dst_ref=pair_recv.at[s],
+            send_sem=pair_ssem.at[s], recv_sem=pair_rsem.at[s],
+            device_id=(partner, chan), device_id_type=MESH,
+        )
+
+    def chip_copy(s):
+        return pltpu.make_async_remote_copy(
+            src_ref=chip_sum.at[s], dst_ref=chip_recv.at[s],
+            send_sem=chip_ssem.at[s], recv_sem=chip_rsem.at[s],
+            device_id=(lax.rem(chip + s + 1, n_chips) * 2 + core, chan), device_id_type=MESH,
+        )
+
+    def forward(s):
+        pair_copy(s).wait()
+        chip_sum[s] = part[core, s] + pair_recv[s]
+        chip_copy(s).start()
+
+    for s in range(n_chips):
+        owner = lax.rem(chip + s + 1, n_chips)
+        columns = pl.ds(pl.multiple_of(owner * (2 * owned), 2 * owned), 2 * owned)
+        chunk = jnp.zeros((features, 2 * owned), jnp.float32)
+        for r in range(rows):
+            chunk = chunk + jnp.dot(masked[r], cot[r, :, columns], preferred_element_type=jnp.float32)
+        part[0, s] = chunk[:, :owned]
+        part[1, s] = chunk[:, owned:]
+        pair_copy(s).start()
+        if s >= 1:
+            forward(s - 1)
+
+    last = n_chips - 1
+    total = count_send[...]
+    for o in range(1, n_lat):
+        count_copies[o - 1].wait()
+        total = total + count_recv[o - 1]
+    scale = lax.rsqrt(jnp.maximum(total.astype(jnp.float32), 1.0))[:1]
+    pair_copy(last).wait()
+    summed = part[core, last] + pair_recv[last]
+    for s in range(n_chips - 1):
+        chip_copy(s).wait()
+        summed = summed + chip_recv[s]
+    wgrad_ref[...] = summed * jnp.broadcast_to(scale[:, :1], summed.shape)
+
+
+def fused(n_lat, n_chan, field, cotangent, weight, lon_counts, point_mask):
+    rows, patches, features = field.shape
+    width = point_mask.shape[1]
+    embed = cotangent.shape[2]
+    owned = embed // n_lat
+    n_chips = n_lat // 2
+    shifts = len({z * width % P_SIZE for z in range(n_chan)})
+    covered = round_up(width // P_SIZE + 2, LANES)
+    padded = max(round_up(patches, LANES), covered)
+    anywhere = pl.BlockSpec(memory_space=pl.ANY)
+    vmem = pl.BlockSpec(memory_space=pltpu.VMEM)
+    dma = pltpu.SemaphoreType.DMA
+    grad, wgrad = pl.pallas_call(
+        functools.partial(kernel, n_lat, n_chan),
+        out_shape=(
+            jax.ShapeDtypeStruct((rows, features, patches), jnp.bfloat16),
+            jax.ShapeDtypeStruct((features, owned), jnp.float32),
+        ),
+        in_specs=[anywhere, anywhere, anywhere, pl.BlockSpec(memory_space=pltpu.SMEM), anywhere],
+        out_specs=(vmem, vmem),
+        scratch_shapes=[
+            pltpu.VMEM((rows, patches, embed), jnp.bfloat16),
+            pltpu.VMEM((rows, features, patches), jnp.bfloat16),
+            pltpu.VMEM((features, embed), jnp.bfloat16),
+            pltpu.VMEM((n_chan, rows, width), jnp.int32),
+            pltpu.VMEM((rows * P_SIZE, padded), jnp.float32),
+            pltpu.VMEM((shifts, width, covered), jnp.bfloat16),
+            pltpu.VMEM((rows, features, patches), jnp.bfloat16),
+            pltpu.VMEM((2, n_chips, features, owned), jnp.float32),
+            pltpu.VMEM((n_chips, features, owned), jnp.float32),
+            pltpu.VMEM((n_chips - 1, features, owned), jnp.float32),
+            pltpu.VMEM((n_chips - 1, features, owned), jnp.float32),
+            pltpu.VMEM((8, LANES), jnp.int32),
+            pltpu.VMEM((n_lat - 1, 8, LANES), jnp.int32),
+            dma((rows,)),
+            dma((3,)),
+            dma((n_chan - 1,)),
+            dma((n_chan - 1,)),
+            dma((n_lat - 1,)),
+            dma((n_lat - 1,)),
+            dma((n_chips,)),
+            dma((n_chips,)),
+            dma((n_chips - 1,)),
+            dma((n_chips - 1,)),
+        ],
+        compiler_params=pltpu.CompilerParams(
+            collective_id=0, has_side_effects=True, vmem_limit_bytes=61 * 1024 * 1024
+        ),
+    )(jnp.swapaxes(field, 1, 2), cotangent, weight, lon_counts, point_mask)
+    return jnp.swapaxes(grad, 1, 2), wgrad.T
+
+
+def plain(field, cotangent, weight, lon_counts, point_mask):
     row_count, patch_count, features = field.shape
     channels = features // P_SIZE
     full_mask = lax.all_gather(point_mask, "chan", axis=1, tiled=True)
@@ -37,6 +249,14 @@
 
 
 def solution(mesh):
+    n_lat, n_chan = mesh.shape["lat"], mesh.shape["chan"]
+
+    def local(field, cotangent, weight, lon_counts, point_mask):
+        whole_tiles = cotangent.shape[2] % (n_lat * LANES) == 0
+        if n_lat % 2 == 0 and n_lat > 2 and n_chan > 1 and whole_tiles:
+            return fused(n_lat, n_chan, field, cotangent, weight, lon_counts, point_mask)
+        return plain(field, cotangent, weight, lon_counts, point_mask)
+
     in_specs = (
         P("lat", None, "chan"),
         P("lat", None, None),

time: 80.1 us -> 25.3 us (0.32)
  waiting for transfers between devices: 25.5 us -> 0 us
  blocking collectives: 24.3 us -> 0 us
  Pallas kernels: 0 us -> 20.7 us
  between operations: 14.8 us -> 0.64 us
  matrix products: 11.3 us -> 0 us
  other arithmetic: 1.4 us -> 0 us
  local copies, waits for them, and re-layouts: 2.58 us -> 3.77 us
    reduce_scatter x1 -> x0, waiting for transfers between devices: 25.5 us -> none  [local(): lax.psum_scatter(summed * scale, 'lat', scatter_dimension=0, tiled=True)]
    pallas_call x0 -> x1, Pallas kernels: none -> 20.7 us  [fused(): pl.pallas_call(functools.partial(kernel, n_lat, n_chan), out_shape=(jax.S...]
    all_gather x1 -> x0, blocking collectives: 15.7 us -> none  [local(): full_mask = lax.all_gather(point_mask, 'chan', axis=1, tiled=True)]
    dot_general x2 -> x0, matrix products: 11.3 us -> none  [the longest x1 6.02 us: local(): lax.dot_general(cotangent, weight, (((2,), (1,)), ((), ())), preferred_el...]
    psum x1 -> x0, blocking collectives: 8.65 us -> none  [local(): total = lax.psum(jnp.sum(valid), 'lat')]
    unnamed x3 -> x2, local copies, waits for them, and re-layouts: 0.15 us -> 3.77 us
    convert_element_type x4 -> x0, local copies, waits for them, and re-layouts: 2.4 us -> none  [the longest x2 1.26 us: local(): point_valid.astype(jnp.float32)]
    reduce_sum x1 -> x0, other arithmetic: 1.4 us -> none  [local(): total = lax.psum(jnp.sum(valid), 'lat')]
  transfers between devices with their start and end apart: 1 -> 0, of which waited for: 1 -> 0; matrix products, arithmetic and copies ran while one was open for 9% -> 0% of each run, Pallas kernels for 0% -> 0%
where the time goes in v1:
time: 25.3 us; the launch traced here: 25.1 us
  Pallas kernels  20.7 us (82%)
  local copies, waits for them, and re-layouts  3.77 us (15%)
  between operations  0.64 us (3%)
    pallas_call x1, Pallas kernels, fused(): pl.pallas_call(functools.partial(kernel, n_lat, n_chan), out_shape=(jax.S...  20.7 us
    unnamed x2, local copies, waits for them, and re-layouts  3.77 us

profile of v1, /device:TPU:0, one launch (start us, length us, event | category | flops | bytes accessed | tf_op | source)
XLA Modules:
  0.0 25.1 jit_solution(15793418307409791906)
XLA Ops:
  0.6 20.7 %shard_map.68 = (bf16[5,136,642]{2,1,0:T(8,128)(2,1)}, f32[136,128]{1,0:T(8,128)}) custom-call(bf16[5,136,642]{2,1,0:T(8,128)(2,1)} %bitcast.3, bf16[5,642,1024]{2,1,0:T(8,128)(2,1)} %cot_hbm.1, bf16[136,1024]{1,0:T(8,128)(2,1)} %weight_hbm.1, s32[5]{0:T(128)} %lon_ref.1, s32[5,1284]{1,0:T(8,128)} %mask_hbm.1), custom_call_target="tpu_custom_call" | custom-call | tf_op jit(solution)/shard_map/pallas_call | solution.py:181
  21.3 2.3 %copy.9 = bf16[5,642,136]{1,2,0:T(8,128)(2,1)} copy(bf16[5,642,136]{1,2,0:T(8,128)(2,1)} %bitcast.4) | data formatting | bytes 1746240
  23.6 1.5 %copy.10 = f32[128,136]{0,1:T(8,128)} copy(f32[128,136]{0,1:T(8,128)} %bitcast.5) | data formatting | bytes 139264

commit v2 on v1

--- a/solution.py
+++ b/solution.py
@@ -18,9 +18,9 @@
 
 def kernel(
     n_lat, n_chan,
-    field_hbm, cot_hbm, weight_hbm, lon_ref, mask_hbm,
+    field_hbm, cot_hbm, weight_hbm, lon_hbm, mask_hbm,
     grad_ref, wgrad_ref,
-    cot, field, weight, masks, expand, spread, masked,
+    cot, field, weight, lon_ref, masks, expand, spread, masked, tiled,
     part, pair_recv, chip_sum, chip_recv, count_send, count_recv,
     cot_sem, load_sem, mask_send, mask_recv, count_ssem, count_rsem,
     pair_ssem, pair_rsem, chip_ssem, chip_rsem,
@@ -35,6 +35,8 @@
 
     load_mask = pltpu.make_async_copy(mask_hbm, masks.at[chan], load_sem.at[0])
     load_mask.start()
+    load_lon = pltpu.make_async_copy(lon_hbm, lon_ref, load_sem.at[3])
+    load_lon.start()
     load_weight = pltpu.make_async_copy(weight_hbm, weight, load_sem.at[1])
     load_weight.start()
     for r in range(rows):
@@ -68,13 +70,19 @@
 
     load_weight.wait()
 
-    @pl.loop(0, rows)
+    early = rows - 2 if rows > 2 else rows
+
+    def product(r):
+        return lax.dot_general(
+            weight[...], cot[r], (((1,), (1,)), ((), ())), preferred_element_type=jnp.float32
+        ).astype(jnp.bfloat16)
+
+    @pl.loop(0, early)
     def _(r):
         pltpu.make_async_copy(cot_hbm.at[r], cot.at[r], cot_sem.at[r]).wait()
-        grad_ref[r] = lax.dot_general(
-            weight[...], cot[r], (((1,), (1,)), ((), ())), preferred_element_type=jnp.float32
-        ).astype(jnp.bfloat16)
-
+        grad_ref[r] = product(r)
+
+    load_lon.wait()
     for copy in mask_copies:
         copy.wait()
 
@@ -107,9 +115,10 @@
     load_field.wait()
     for r in range(rows):
         valid8 = expand[r * P_SIZE:(r + 1) * P_SIZE, :patches]
-        tiled = jnp.concatenate([valid8] * (features // P_SIZE), axis=0).astype(jnp.bfloat16)
-        masked[r] = field[r] * tiled
-        grad_ref[r] = grad_ref[r] * tiled
+        tiled[r] = jnp.concatenate([valid8] * (features // P_SIZE), axis=0).astype(jnp.bfloat16)
+        masked[r] = field[r] * tiled[r]
+    for r in range(early, rows):
+        pltpu.make_async_copy(cot_hbm.at[r], cot.at[r], cot_sem.at[r]).wait()
 
     count_copies = []
     for o in range(1, n_lat):
@@ -151,6 +160,14 @@
         pair_copy(s).start()
         if s >= 1:
             forward(s - 1)
+
+    @pl.loop(early, rows)
+    def _(r):
+        grad_ref[r] = product(r) * tiled[r]
+
+    @pl.loop(0, early)
+    def _(r):
+        grad_ref[r] = grad_ref[r] * tiled[r]
 
     last = n_chips - 1
     total = count_send[...]
@@ -166,6 +183,17 @@
     wgrad_ref[...] = summed * jnp.broadcast_to(scale[:, :1], summed.shape)
 
 
+def write_out(grad_ref, wgrad_ref, grad_hbm, wgrad_hbm, sem):
+    copies = [
+        pltpu.make_async_copy(grad_ref, grad_hbm, sem.at[0]),
+        pltpu.make_async_copy(wgrad_ref, wgrad_hbm, sem.at[1]),
+    ]
+    for copy in copies:
+        copy.start()
+    for copy in copies:
+        copy.wait()
+
+
 def fused(n_lat, n_chan, field, cotangent, weight, lon_counts, point_mask):
     rows, patches, features = field.shape
     width = point_mask.shape[1]
@@ -175,7 +203,7 @@
     shifts = len({z * width % P_SIZE for z in range(n_chan)})
     covered = round_up(width // P_SIZE + 2, LANES)
     padded = max(round_up(patches, LANES), covered)
-    anywhere = pl.BlockSpec(memory_space=pl.ANY)
+    anywhere = pl.BlockSpec(memory_space=pltpu.HBM)
     vmem = pl.BlockSpec(memory_space=pltpu.VMEM)
     dma = pltpu.SemaphoreType.DMA
     grad, wgrad = pl.pallas_call(
@@ -184,15 +212,17 @@
             jax.ShapeDtypeStruct((rows, features, patches), jnp.bfloat16),
             jax.ShapeDtypeStruct((features, owned), jnp.float32),
         ),
-        in_specs=[anywhere, anywhere, anywhere, pl.BlockSpec(memory_space=pltpu.SMEM), anywhere],
+        in_specs=[anywhere] * 5,
         out_specs=(vmem, vmem),
         scratch_shapes=[
             pltpu.VMEM((rows, patches, embed), jnp.bfloat16),
             pltpu.VMEM((rows, features, patches), jnp.bfloat16),
             pltpu.VMEM((features, embed), jnp.bfloat16),
+            pltpu.SMEM((rows,), jnp.int32),
             pltpu.VMEM((n_chan, rows, width), jnp.int32),
             pltpu.VMEM((rows * P_SIZE, padded), jnp.float32),
             pltpu.VMEM((shifts, width, covered), jnp.bfloat16),
+            pltpu.VMEM((rows, features, patches), jnp.bfloat16),
             pltpu.VMEM((rows, features, patches), jnp.bfloat16),
             pltpu.VMEM((2, n_chips, features, owned), jnp.float32),
             pltpu.VMEM((n_chips, features, owned), jnp.float32),
@@ -201,7 +231,7 @@
             pltpu.VMEM((8, LANES), jnp.int32),
             pltpu.VMEM((n_lat - 1, 8, LANES), jnp.int32),
             dma((rows,)),
-            dma((3,)),
+            dma((4,)),
             dma((n_chan - 1,)),
             dma((n_chan - 1,)),
             dma((n_lat - 1,)),
@@ -212,9 +242,26 @@
             dma((n_chips - 1,)),
         ],
         compiler_params=pltpu.CompilerParams(
-            collective_id=0, has_side_effects=True, vmem_limit_bytes=61 * 1024 * 1024
+            collective_id=0, has_side_effects=True, vmem_limit_bytes=24 * 1024 * 1024
         ),
-    )(jnp.swapaxes(field, 1, 2), cotangent, weight, lon_counts, point_mask)
+    )(
+        pltpu.with_memory_space_constraint(jnp.swapaxes(field, 1, 2), pltpu.HBM),
+        pltpu.with_memory_space_constraint(cotangent, pltpu.HBM),
+        pltpu.with_memory_space_constraint(weight, pltpu.HBM),
+        pltpu.with_memory_space_constraint(lon_counts, pltpu.HBM),
+        pltpu.with_memory_space_constraint(point_mask, pltpu.HBM),
+    )
+    grad, wgrad = pl.pallas_call(
+        write_out,
+        out_shape=(
+            jax.ShapeDtypeStruct(grad.shape, grad.dtype),
+            jax.ShapeDtypeStruct(wgrad.shape, wgrad.dtype),
+        ),
+        in_specs=[vmem, vmem],
+        out_specs=(anywhere, anywhere),
+        scratch_shapes=[dma((2,))],
+        compiler_params=pltpu.CompilerParams(vmem_limit_bytes=4 * 1024 * 1024),
+    )(grad, wgrad)
     return jnp.swapaxes(grad, 1, 2), wgrad.T
 
 

time: 25.3 us -> 20.6 us (0.81)
  local copies, waits for them, and re-layouts: 3.77 us -> 0 us
  Pallas kernels: 20.7 us -> 19.8 us
    unnamed x2 -> x0, local copies, waits for them, and re-layouts: 3.77 us -> none
    pallas_call x1, Pallas kernels: 20.7 us -> 18.8 us  [fused(): pl.pallas_call(functools.partial(kernel, n_lat, n_chan), out_shape=(jax.S...]
    pallas_call x0 -> x1, Pallas kernels: none -> 0.99 us  [fused(): pl.pallas_call(write_out, out_shape=(jax.ShapeDtypeStruct(grad.shape, gra...]
where the time goes in v2:
time: 20.6 us; the launch traced here: 20.5 us
  Pallas kernels  19.8 us (96%)
  between operations  0.64 us (3%)
    pallas_call x1, Pallas kernels, fused(): pl.pallas_call(functools.partial(kernel, n_lat, n_chan), out_shape=(jax.S...  18.8 us
    pallas_call x1, Pallas kernels, fused(): pl.pallas_call(write_out, out_shape=(jax.ShapeDtypeStruct(grad.shape, gra...  0.99 us

profile of v2, /device:TPU:0, one launch (start us, length us, event | category | flops | bytes accessed | tf_op | source)
XLA Modules:
  0.0 20.5 jit_solution(16160440500324022750)
XLA Ops:
  0.6 18.8 %shard_map.68 = (bf16[5,136,642]{2,1,0:T(8,128)(2,1)S(1)}, f32[136,128]{1,0:T(8,128)S(1)}) custom-call(bf16[5,136,642]{2,1,0:T(8,128)(2,1)} %bitcast.3, bf16[5,642,1024]{2,1,0:T(8,128)(2,1)} %cot_hbm.1, bf16[136,1024]{1,0:T(8,128)(2,1)} %weight_hbm.1, s32[5]{0:T(128)} %lon_hbm.1, s32[5,1284]{1,0:T(8,128)} %mask_hbm.1), custom_call_target="tpu_custom_call" | custom-call | tf_op jit(solution)/shard_map/pallas_call | solution.py:209
  19.5 1.0 %shard_map.69 = (bf16[5,136,642]{2,1,0:T(8,128)(2,1)}, f32[136,128]{1,0:T(8,128)}) custom-call(bf16[5,136,642]{2,1,0:T(8,128)(2,1)S(1)} %get-tuple-element.6.grad_ref, f32[136,128]{1,0:T(8,128)S(1)} %get-tuple-element.7.wgrad_ref), custom_call_target="tpu_custom_call" | custom-call | tf_op jit(solution)/shard_map/pallas_call | solution.py:254

commit v3 on v2

--- a/solution.py
+++ b/solution.py
@@ -14,6 +14,15 @@
 
 def round_up(value, multiple):
     return (value + multiple - 1) // multiple * multiple
+
+
+def flip(index, bits):
+    result, bit = index, 1
+    while bit <= bits:
+        if bits & bit:
+            result = result + bit * (1 - 2 * lax.rem(lax.div(index, bit), 2))
+        bit *= 2
+    return result
 
 
 def kernel(
@@ -30,8 +39,8 @@
     n_chips = n_lat // 2
     owned = wgrad_ref.shape[1]
     lat, chan = lax.axis_index("lat"), lax.axis_index("chan")
-    chip, core = lat // 2, lax.rem(lat, 2)
-    partner = chip * 2 + 1 - core
+    chip, core = lax.div(lat, 2), lax.rem(lat, 2)
+    partner = flip(lat, 1)
 
     load_mask = pltpu.make_async_copy(mask_hbm, masks.at[chan], load_sem.at[0])
     load_mask.start()
@@ -46,9 +55,9 @@
 
     barrier = pltpu.get_barrier_semaphore()
     for o in range(1, n_chan):
-        pl.semaphore_signal(barrier, inc=1, device_id=(lat, lax.rem(chan + o, n_chan)), device_id_type=MESH)
+        pl.semaphore_signal(barrier, inc=1, device_id=(lat, flip(chan, o)), device_id_type=MESH)
     for o in range(1, n_lat):
-        pl.semaphore_signal(barrier, inc=1, device_id=(lax.rem(lat + o, n_lat), chan), device_id_type=MESH)
+        pl.semaphore_signal(barrier, inc=1, device_id=(flip(lat, o), chan), device_id_type=MESH)
 
     lane_of = lax.broadcasted_iota(jnp.int32, spread.shape[1:], 0)
     patch_of = lax.broadcasted_iota(jnp.int32, spread.shape[1:], 1)
@@ -58,15 +67,15 @@
 
     load_mask.wait()
     pl.semaphore_wait(barrier, n_chan + n_lat - 2)
-    mask_copies = []
-    for o in range(1, n_chan):
+    mask_copies = {}
+    for o in reversed(range(1, n_chan)):
         copy = pltpu.make_async_remote_copy(
             src_ref=masks.at[chan], dst_ref=masks.at[chan],
             send_sem=mask_send.at[o - 1], recv_sem=mask_recv.at[o - 1],
-            device_id=(lat, lax.rem(chan + o, n_chan)), device_id_type=MESH,
+            device_id=(lat, flip(chan, o)), device_id_type=MESH,
         )
         copy.start()
-        mask_copies.append(copy)
+        mask_copies[o] = copy
 
     load_weight.wait()
 
@@ -83,31 +92,31 @@
         grad_ref[r] = product(r)
 
     load_lon.wait()
-    for copy in mask_copies:
-        copy.wait()
-
     padded = expand.shape[1]
     lane = lax.broadcasted_iota(jnp.int32, (P_SIZE, width), 1)
     sub = lax.broadcasted_iota(jnp.int32, (P_SIZE, width), 0)
     counts = jnp.zeros((1, width), jnp.int32)
     valid_all = jnp.zeros((rows * P_SIZE, padded), jnp.float32)
-    for z in range(n_chan):
-        first, shift = z * width // P_SIZE, z * width % P_SIZE
+    for o in range(n_chan):
+        if o > 0:
+            mask_copies[o].wait_recv()
+        z = flip(chan, o)
+        first, shift = lax.div(z * width, P_SIZE), lax.rem(z * width, P_SIZE)
+        kind = sum((z == other).astype(jnp.int32) * shifts.index(other * width % P_SIZE) for other in range(n_chan))
         pick = lax.rem(lane + shift, P_SIZE) == sub
         position = lane[:1] + z * width
-        block = masks[z]
         placed = []
         for r in range(rows):
-            valid = jnp.where(position < lon_ref[r], block[r:r + 1], 0)
+            valid = jnp.where(position < lon_ref[r], masks[z, r:r + 1], 0)
             counts = counts + valid
             placed.append(jnp.where(pick, jnp.broadcast_to(valid, (P_SIZE, width)), 0))
         left = jnp.concatenate(placed, axis=0).astype(jnp.float32).astype(jnp.bfloat16)
-        local = jnp.dot(left, spread[shifts.index(shift)], preferred_element_type=jnp.float32)
+        local = jnp.dot(left, spread[kind], preferred_element_type=jnp.float32)
         if padded > local.shape[1]:
             local = jnp.concatenate(
                 [local, jnp.zeros((rows * P_SIZE, padded - local.shape[1]), jnp.float32)], axis=1
             )
-        valid_all = valid_all + (pltpu.roll(local, first, axis=1) if first else local)
+        valid_all = valid_all + pltpu.roll(local, first, axis=1)
     expand[...] = valid_all
     total_here = jnp.sum(counts)
     count_send[...] = jnp.full(count_send.shape, total_here, jnp.int32)
@@ -125,7 +134,7 @@
         copy = pltpu.make_async_remote_copy(
             src_ref=count_send, dst_ref=count_recv.at[o - 1],
             send_sem=count_ssem.at[o - 1], recv_sem=count_rsem.at[o - 1],
-            device_id=(lax.rem(lat + o, n_lat), chan), device_id_type=MESH,
+            device_id=(flip(lat, o), chan), device_id_type=MESH,
         )
         copy.start()
         count_copies.append(copy)
@@ -141,16 +150,16 @@
         return pltpu.make_async_remote_copy(
             src_ref=chip_sum.at[s], dst_ref=chip_recv.at[s],
             send_sem=chip_ssem.at[s], recv_sem=chip_rsem.at[s],
-            device_id=(lax.rem(chip + s + 1, n_chips) * 2 + core, chan), device_id_type=MESH,
+            device_id=(flip(chip, n_chips - 1 - s) * 2 + core, chan), device_id_type=MESH,
         )
 
     def forward(s):
-        pair_copy(s).wait()
+        pair_copy(s).wait_recv()
         chip_sum[s] = part[core, s] + pair_recv[s]
         chip_copy(s).start()
 
     for s in range(n_chips):
-        owner = lax.rem(chip + s + 1, n_chips)
+        owner = flip(chip, n_chips - 1 - s)
         columns = pl.ds(pl.multiple_of(owner * (2 * owned), 2 * owned), 2 * owned)
         chunk = jnp.zeros((features, 2 * owned), jnp.float32)
         for r in range(rows):
@@ -158,8 +167,10 @@
         part[0, s] = chunk[:, :owned]
         part[1, s] = chunk[:, owned:]
         pair_copy(s).start()
-        if s >= 1:
-            forward(s - 1)
+        if s == n_chips - 2:
+            forward(0)
+    for s in range(1, n_chips - 1):
+        forward(s)
 
     @pl.loop(early, rows)
     def _(r):
@@ -175,6 +186,10 @@
         count_copies[o - 1].wait()
         total = total + count_recv[o - 1]
     scale = lax.rsqrt(jnp.maximum(total.astype(jnp.float32), 1.0))[:1]
+    for s in range(last):
+        pair_copy(s).wait_send()
+    for o in range(1, n_chan):
+        mask_copies[o].wait_send()
     pair_copy(last).wait()
     summed = part[core, last] + pair_recv[last]
     for s in range(n_chips - 1):
@@ -300,7 +315,8 @@
 
     def local(field, cotangent, weight, lon_counts, point_mask):
         whole_tiles = cotangent.shape[2] % (n_lat * LANES) == 0
-        if n_lat % 2 == 0 and n_lat > 2 and n_chan > 1 and whole_tiles:
+        powers = n_lat & (n_lat - 1) == 0 and n_chan & (n_chan - 1) == 0
+        if powers and n_lat > 2 and n_chan > 1 and whole_tiles:
             return fused(n_lat, n_chan, field, cotangent, weight, lon_counts, point_mask)
         return plain(field, cotangent, weight, lon_counts, point_mask)
 

time: 20.6 us -> 21.7 us (1.053)
  Pallas kernels: 19.8 us -> 20.9 us
    pallas_call x1, Pallas kernels: 18.8 us -> 19.9 us  [fused(): pl.pallas_call(functools.partial(kernel, n_lat, n_chan), out_shape=(jax.S...]
where the time goes in v3:
time: 21.7 us; the launch traced here: 21.5 us
  Pallas kernels  20.9 us (96%)
  between operations  0.64 us (3%)
    pallas_call x1, Pallas kernels, fused(): pl.pallas_call(functools.partial(kernel, n_lat, n_chan), out_shape=(jax.S...  19.9 us
    pallas_call x1, Pallas kernels, fused(): pl.pallas_call(write_out, out_shape=(jax.ShapeDtypeStruct(grad.shape, gra...  0.99 us

profile of v3, /device:TPU:0, one launch (start us, length us, event | category | flops | bytes accessed | tf_op | source)
XLA Modules:
  0.0 21.5 jit_solution(17381503538484945488)
XLA Ops:
  0.6 19.9 %shard_map.68 = (bf16[5,136,642]{2,1,0:T(8,128)(2,1)S(1)}, f32[136,128]{1,0:T(8,128)S(1)}) custom-call(bf16[5,136,642]{2,1,0:T(8,128)(2,1)} %bitcast.3, bf16[5,642,1024]{2,1,0:T(8,128)(2,1)} %cot_hbm.1, bf16[136,1024]{1,0:T(8,128)(2,1)} %weight_hbm.1, s32[5]{0:T(128)} %lon_hbm.1, s32[5,1284]{1,0:T(8,128)} %mask_hbm.1), custom_call_target="tpu_custom_call" | custom-call | tf_op jit(solution)/shard_map/pallas_call | solution.py:224
  20.5 1.0 %shard_map.69 = (bf16[5,136,642]{2,1,0:T(8,128)(2,1)}, f32[136,128]{1,0:T(8,128)}) custom-call(bf16[5,136,642]{2,1,0:T(8,128)(2,1)S(1)} %get-tuple-element.6.grad_ref, f32[136,128]{1,0:T(8,128)S(1)} %get-tuple-element.7.wgrad_ref), custom_call_target="tpu_custom_call" | custom-call | tf_op jit(solution)/shard_map/pallas_call | solution.py:269
